TPU v7x, 32 devices: a whole 2x2x4 slice. The times are simulated.
32 devices in a mesh: blk: 16 (over z, y, core), dp: 2 (over x).
Axes of the slice: x: 2, y: 2, z: 4, core: 2. Of those that a mesh axis runs over, the one named last changes fastest.
Arguments:
- query_feats: bfloat16 [2, 6144, 1024], P('dp', 'blk'), may hold values from -12 to 12
- item_feats: bfloat16 [2, 6144, 1024], P('dp', 'blk'), may hold values from -12 to 12
- item_ids: int32 [2, 6144], P('dp', 'blk'), may hold values from 0 to 1048575
- bucket_ids: int32 [2, 6144], P('dp', 'blk'), may hold values from 0 to 255
- bucket_logq: float32 [256], replicated, may hold values from -7 to -5.5
- query_tower: bfloat16 [1024, 256], replicated, may hold values from -0.1875 to 0.1875
- item_tower: bfloat16 [1024, 256], replicated, may hold values from -0.1875 to 0.1875
Outputs:
- grad_query_tower: float32 [1024, 256], replicated
- grad_item_tower: float32 [1024, 256], replicated
- loss: float32 [], replicated
All inputs are finite; a program needn't handle non-finite values.
Results may differ from a plain program's by a relative error of at most 0.0041.
Values may be sent and summed in bfloat16 or wider, within the bound.
A program may use at most 128 MiB of HBM per device.

v0:
```python
import math
import jax
import jax.numpy as jnp
from jax import lax
from jax.sharding import PartitionSpec as P

EXCLUDED = -1e30


def contract_last(left, right):
    return lax.dot_general(
        left, right, (((1,), (1,)), ((), ())), preferred_element_type=jnp.float32
    )


def contract_first(left, right):
    return lax.dot_general(
        left, right, (((0,), (0,)), ((), ())), preferred_element_type=jnp.float32
    )


def on_device(query_feats, item_feats, item_ids, bucket_ids, bucket_logq, query_tower, item_tower):
    query_input = query_feats[0]
    item_input = item_feats[0]
    own_ids = item_ids[0]
    local_rows = query_input.shape[0]
    embed_width = query_tower.shape[1]
    scaling = 1.0 / math.sqrt(embed_width)
    query_vecs = jnp.dot(query_input, query_tower, preferred_element_type=jnp.float32).astype(
        jnp.bfloat16
    )
    item_vecs = jnp.dot(item_input, item_tower, preferred_element_type=jnp.float32).astype(
        jnp.bfloat16
    )
    all_items = lax.all_gather(item_vecs, "blk", axis=0, tiled=True)
    all_ids, all_buckets = (
        lax.all_gather(own_ids, "blk", axis=0, tiled=True),
        lax.all_gather(bucket_ids[0], "blk", axis=0, tiled=True),
    )
    group_size = all_ids.shape[0]
    bucket_range = jnp.arange(bucket_logq.shape[0], dtype=jnp.int32)
    correction = jnp.sum(
        jnp.where(all_buckets[:, None] == bucket_range[None, :], bucket_logq[None, :], 0.0), axis=1
    )
    offset = lax.axis_index("blk") * local_rows
    rows_global = offset + jnp.arange(local_rows, dtype=jnp.int32)
    columns = jnp.arange(group_size, dtype=jnp.int32)
    scores = contract_last(query_vecs, all_items) * scaling - correction[None, :]
    duplicate = (all_ids[None, :] == own_ids[:, None]) & (columns[None, :] != rows_global[:, None])
    masked = jnp.where(duplicate, EXCLUDED, scores)
    peaks = jnp.max(masked, axis=1)
    log_total = peaks + jnp.log(jnp.sum(jnp.exp(masked - peaks[:, None]), axis=1))
    softmax = jnp.exp(masked - log_total[:, None]).astype(jnp.bfloat16)
    positive = jnp.diagonal(lax.dynamic_slice_in_dim(scores, offset, local_rows, 1))
    loss_local = jnp.sum(log_total - positive)
    query_grad = (
        (
            jnp.dot(softmax, all_items, preferred_element_type=jnp.float32)
            - item_vecs.astype(jnp.float32)
        )
        * scaling
    ).astype(jnp.bfloat16)
    tower_query = contract_first(query_input, query_grad)
    all_totals = lax.all_gather(log_total, "blk", axis=0, tiled=True)
    own_correction = lax.dynamic_slice_in_dim(correction, offset, local_rows, 0)
    shard_rows = lax.all_gather(query_vecs, "blk", axis=0, tiled=True)
    row_count = shard_rows.shape[0]
    piece_rows = jnp.arange(row_count, dtype=jnp.int32)
    piece_scores = contract_last(shard_rows, item_vecs) * scaling - own_correction[None, :]
    piece_dup = (own_ids[None, :] == all_ids[:, None]) & (
        rows_global[None, :] != piece_rows[:, None]
    )
    piece_masked = jnp.where(piece_dup, EXCLUDED, piece_scores)
    piece_soft = jnp.exp(piece_masked - all_totals[:, None]).astype(jnp.bfloat16)
    item_sums = contract_first(piece_soft, shard_rows)
    item_grad = ((item_sums - query_vecs.astype(jnp.float32)) * scaling).astype(jnp.bfloat16)
    tower_item = contract_first(item_input, item_grad)
    grad_query, grad_item, loss_total = lax.psum(
        (tower_query, tower_item, loss_local), ("blk", "dp")
    )
    loss = loss_total / (lax.axis_size("dp") * group_size)
    return (grad_query, grad_item, loss)


def solution(mesh):
    return jax.shard_map(
        on_device,
        mesh=mesh,
        in_specs=(
            P("dp", "blk", None),
            P("dp", "blk", None),
            P("dp", "blk"),
            P("dp", "blk"),
            P(),
            P(),
            P(),
        ),
        out_specs=(P(), P(), P()),
        check_vma=False,
    )
```

profile of v0, /device:TPU:0, one launch (start us, length us, event | category | flops | bytes accessed | tf_op | source)
XLA Modules:
  0.0 271.1 jit_solution(16974433415751441784)
XLA Ops:
  7.2 0.0 copy-start
  7.2 0.0 all-gather.6.cloned.1.call-start
  7.2 1.1 copy-done
  8.3 2.1 convolution_convert_fusion
  10.4 0.0 all-gather.6.cloned.1.call-update
  10.4 0.0 all-gather.8.cloned.1.call-start
  10.5 2.3 convolution_convert_fusion.1
  12.8 0.0 all-gather.8.cloned.1.call-update
  12.8 0.0 all-reduce.3.cloned.1.call-start
  12.9 0.7 reduce
  13.6 23.4 %all-gather.1 = s32[1,6144]{1,0:T(1,128)S(1)} all-gather(s32[1,384]{1,0:T(1,128)} %param.10), channel_id=3, replica_groups=mesh['blk'=16,'dp'=2] {'blk'}, dimensions={1}, use_global_device_ids=true | all-gather | bytes 26112 | tf_op jit(solution)/shard_map/all_gather | solution.py:38
  37.0 4.4 %select_reduce_fusion = f32[6144]{0:T(1024)S(1)} fusion(f32[256]{0:T(256)} %param.11, s32[6144]{0:T(1024)S(1)} %bitcast.30), kind=kLoop, calls=%fused_computation.10 | loop fusion | flops 4712448 | bytes 50176 | tf_op jit(solution)/shard_map/reduce_sum | solution.py:42
  41.4 0.1 dynamic_slice.6
  41.5 18.0 %all-gather = s32[1,6144]{1,0:T(1,128)S(1)} all-gather(s32[1,384]{1,0:T(1,128)} %param.9), channel_id=2, replica_groups=mesh['blk'=16,'dp'=2] {'blk'}, dimensions={1}, use_global_device_ids=true | all-gather | bytes 26112 | tf_op jit(solution)/shard_map/all_gather | solution.py:37
  59.5 0.0 all-gather.6.cloned.1.call-done
  59.5 5.1 %fusion.3 = (f32[384]{0:T(512)S(1)}, f32[384,6144]{1,0:T(8,128)S(1)}) fusion(s32[384]{0:T(512)S(1)} %iota_add_fusion, s32[6144]{0:T(1024)S(1)} %bitcast.26, s32[384]{0:T(512)S(1)} %reduce, f32[6144]{0:T(1024)S(1)} %select_reduce_fusion, bf16[384,256]{1,0:T(8,128)(2,1)} %convolution_convert_fusion.1, bf16[6144,256]{1,0:T(8,128)(2,1)} %all-gather.6.cloned.1.call-done), kind=kOutput, calls=%fused_computation.12 | convolution fusion | flops 1224474240 | bytes 12833280 | tf_op jit(solution)/shard_map/dot_general | solution.py:11
  64.6 0.0 copy-start.1
  64.6 0.0 copy-start.3
  64.6 0.0 copy-start.4
  64.6 3.6 %copy-done.1 = f32[384,6144]{1,0:T(8,128)} copy-done((f32[384,6144]{1,0:T(8,128)}, f32[384,6144]{1,0:T(8,128)S(1)}, u32[]{:S(2)}) %copy-start.1) | copy-done | bytes 9437208
  68.2 0.1 constant_dynamic-slice_fusion
  68.3 3.4 %gather_fusion = f32[384]{0:T(512)S(1)} fusion(f32[384,384]{1,0:T(8,128)S(1)} %constant_dynamic-slice_fusion, s32[384]{0:T(512)S(1)} %or_reduce_fusion), kind=kCustom, calls=%fused_computation | custom fusion | bytes 6144 | tf_op jit(solution)/shard_map/jit(diagonal)/cond/branch_0_fun/gather | solution.py:54
  71.7 6.0 %exponential_reduce_fusion = f32[384]{0:T(512)S(1)} fusion(f32[384,6144]{1,0:T(8,128)} %copy-done.1, f32[384]{0:T(512)S(1)} %get-tuple-element.19, s32[384]{0:T(512)S(1)} %iota_add_fusion, s32[6144]{0:T(1024)S(1)} %bitcast.27, s32[384]{0:T(512)S(1)} %reduce), kind=kLoop, calls=%fused_computation.4 | loop fusion | flops 14155392 | bytes 9467904 | tf_op jit(solution)/shard_map/reduce_sum | solution.py:52
  77.7 0.6 subtract_reduce_fusion
  78.3 19.5 %all-gather.2 = f32[16,1,384]{2,1,0:T(1,128)S(1)} all-gather(f32[1,1,384]{2,1,0:T(1,128)S(1)} %reshape.37), channel_id=1, replica_groups=mesh['blk'=16,'dp'=2] {'blk'}, dimensions={0}, use_global_device_ids=true | all-gather | bytes 26112 | tf_op jit(solution)/shard_map/all_gather | solution.py:64
  97.8 8.1 %all-gather.8.cloned.1.call-done = bf16[6144,256]{1,0:T(8,128)(2,1)} async-done(((bf16[384,256]{1,0:T(8,128)(2,1)}), bf16[6144,256]{1,0:T(8,128)(2,1)}) %all-gather.8.cloned.1.call-update) | async-done | bytes 3145744 | tf_op jit(solution)/shard_map/all_gather | solution.py:66
  105.9 0.0 copy-done.3
  105.9 0.0 copy-done.4
  105.9 0.0 copy-start.2
  105.9 8.5 %fusion.11 = bf16[384,256]{1,0:T(8,128)(2,1)S(1)} fusion(bf16[6144,256]{1,0:T(8,128)(2,1)} %all-gather.8.cloned.1.call-done, bf16[384,256]{1,0:T(8,128)(2,1)S(1)} %copy-done.3, f32[6144]{0:T(1024)S(1)} %bitcast.31, f32[384]{0:T(512)S(1)} %dynamic_slice.6, s32[384]{0:T(512)S(1)} %iota_add_fusion, s32[384]{0:T(512)S(1)} %reduce, s32[6144]{0:T(1024)S(1)} %bitcast.28, ...), kind=kOutput, calls=%fused_computation.24 | convolution fusion | flops 2435186688 | bytes 3789312 | tf_op jit(solution)/shard_map/dot_general | solution.py:17
  114.4 1.4 convolution_bitcast_fusion
  115.8 0.0 copy-done.2
  115.8 9.0 %convolution_bitcast_fusion.1 = f32[1024,256]{0,1:T(8,128)} fusion(bf16[6144,256]{1,0:T(8,128)(2,1)} %all-gather.6.cloned.1.call-done, f32[384,6144]{1,0:T(8,128)} %copy-done.1, f32[384]{0:T(512)S(1)} %get-tuple-element.18, s32[384]{0:T(512)S(1)} %iota_add_fusion, s32[6144]{0:T(1024)S(1)} %bitcast.29, s32[384]{0:T(512)S(1)} %reduce, ...), kind=kOutput, calls=%fused_computation.16 | convolution fusion | flops 1423835136 | bytes 14643712 | tf_op jit(solution)/shard_map/dot_general | solution.py:17
  124.8 0.0 all-reduce.3.cloned.1.call-update
  124.9 39.8 %psum.23 = f32[]{:T(128)} all-reduce(f32[]{:T(128)} %get-tuple-element.17), channel_id=1, replica_groups=mesh['blk'=16,'dp'=2] {'blk','dp'}, use_global_device_ids=true, to_apply=%region_6.7 | all-reduce | flops 1 | bytes 8 | tf_op jit(solution)/shard_map/psum | solution.py:78
  165.3 93.1 %all-reduce.3.cloned.1.call-done = (f32[1024,256]{0,1:T(8,128)}, f32[1024,256]{0,1:T(8,128)}) async-done(((f32[1024,256]{0,1:T(8,128)}, f32[1024,256]{0,1:T(8,128)}), (f32[1024,256]{0,1:T(8,128)}, f32[1024,256]{0,1:T(8,128)})) %all-reduce.3.cloned.1.call-update) | async-done | bytes 2097168 | tf_op jit(solution)/shard_map/psum | solution.py:78
  258.4 2.5 copy.16
  260.9 2.5 copy.17
  (3 shorter events, 0.0 us)
Async XLA Ops:
  7.2 1.1 copy-start
  7.2 52.3 %all-gather.6.cloned.1.call-start = ((), (), s32[]{:S(2)}) async-start(), calls=%async_computation | async-start | bytes 3342336 | tf_op jit(solution)/shard_map/all_gather | solution.py:35
  10.4 95.5 %all-gather.8.cloned.1.call-start = ((), (), s32[]{:S(2)}) async-start(), calls=%async_computation.1 | async-start | bytes 3342336 | tf_op jit(solution)/shard_map/all_gather | solution.py:66
  12.8 245.6 %all-reduce.3.cloned.1.call-start = ((), (), s32[]{:S(2)}) async-start(), calls=%async_computation.2 | async-start | bytes 4194304 | tf_op jit(solution)/shard_map/psum | solution.py:78
  64.6 3.6 %copy-start.1 = (f32[384,6144]{1,0:T(8,128)}, f32[384,6144]{1,0:T(8,128)S(1)}, u32[]{:S(2)}) copy-start(f32[384,6144]{1,0:T(8,128)S(1)} %get-tuple-element.20) | copy-start | bytes 28311556
  64.6 41.3 %copy-start.3 = (bf16[384,256]{1,0:T(8,128)(2,1)S(1)}, bf16[384,256]{1,0:T(8,128)(2,1)}, u32[]{:S(2)}) copy-start(bf16[384,256]{1,0:T(8,128)(2,1)} %convolution_convert_fusion) | copy-start | bytes 589828
  64.6 41.3 %copy-start.4 = (bf16[384,256]{1,0:T(8,128)(2,1)S(1)}, bf16[384,256]{1,0:T(8,128)(2,1)}, u32[]{:S(2)}) copy-start(bf16[384,256]{1,0:T(8,128)(2,1)} %convolution_convert_fusion.1) | copy-start | bytes 589828
  105.9 9.9 %copy-start.2 = (bf16[1,384,1024]{2,1,0:T(8,128)(2,1)S(1)}, bf16[1,384,1024]{2,1,0:T(8,128)(2,1)}, u32[]{:S(2)}) copy-start(bf16[1,384,1024]{2,1,0:T(8,128)(2,1)} %param.7) | copy-start | bytes 2359300
Sparse Core Ops, SparseCore 0:
  10.8 48.2 all-gather.5
  62.0 43.8 all-gather.7
  125.0 133.3 all-reduce.2
where the time goes:
time: 272 us; the launch traced here: 271 us
  waiting for transfers between devices  101 us (37%)
  blocking collectives  101 us (37%)
  matrix products  28.4 us (10%)
  between operations  15.6 us (6%)
  local copies, waits for them, and re-layouts  13.3 us (5%)
  other arithmetic  11.7 us (4%)
    psum x1, waiting for transfers between devices, on_device(): lax.psum((tower_query, tower_item, loss_local), ('blk', 'dp'))  93.1 us
    psum x1, blocking collectives, on_device(): lax.psum((tower_query, tower_item, loss_local), ('blk', 'dp'))  39.8 us
    all_gather x1, blocking collectives, on_device(): lax.all_gather(bucket_ids[0], 'blk', axis=0, tiled=True)  23.4 us
    all_gather x1, blocking collectives, on_device(): all_totals = lax.all_gather(log_total, 'blk', axis=0, tiled=True)  19.5 us
    dot_general x3, matrix products, contract_first(): lax.dot_general(left, right, (((0,), (0,)), ((), ())), preferred_element_...  18.9 us
    all_gather x1, blocking collectives, on_device(): lax.all_gather(own_ids, 'blk', axis=0, tiled=True)  18 us
    unnamed x13, local copies, waits for them, and re-layouts  9.76 us
    all_gather x1, waiting for transfers between devices, on_device(): shard_rows = lax.all_gather(query_vecs, 'blk', axis=0, tiled=True)  8.09 us
  transfers between devices with their start and end apart: 3, of which 2 were waited for; matrix products, arithmetic and copies ran while one was open for 8% of the time, Pallas kernels for 0%

commit v1 on v0

--- a/solution.py
+++ b/solution.py
@@ -76,7 +76,7 @@
     item_grad = ((item_sums - query_vecs.astype(jnp.float32)) * scaling).astype(jnp.bfloat16)
     tower_item = contract_first(item_input, item_grad)
     grad_query, grad_item, loss_total = lax.psum(
-        (tower_query, tower_item, loss_local), ("blk", "dp")
+        lax.psum((tower_query, tower_item, loss_local), "dp"), "blk"
     )
     loss = loss_total / (lax.axis_size("dp") * group_size)
     return (grad_query, grad_item, loss)

time: 272 us -> 301 us (1.11)
  waiting for transfers between devices: 101 us -> 132 us
    psum x1 -> x2, waiting for transfers between devices: 93.1 us -> 124 us  [the longest x1 62.5 us: on_device(): lax.psum(lax.psum((tower_query, tower_item, loss_local), 'dp'), 'blk')]
    psum x1 -> x2, blocking collectives: 39.8 us -> 38.7 us  [the longest x1 33.2 us: on_device(): lax.psum(lax.psum((tower_query, tower_item, loss_local), 'dp'), 'blk')]
  transfers between devices with their start and end apart: 3 -> 4, of which waited for: 2 -> 3; matrix products, arithmetic and copies ran while one was open for 8% -> 8% of each run, Pallas kernels for 0% -> 0%
where the time goes in v1:
time: 301 us
  waiting for transfers between devices  132 us (44%)
  blocking collectives  99.7 us (33%)
  matrix products  28.4 us (9%)
  between operations  15.6 us (5%)
  local copies, waits for them, and re-layouts  13.3 us (4%)
  other arithmetic  11.7 us (4%)
    psum x1, waiting for transfers between devices, on_device(): lax.psum(lax.psum((tower_query, tower_item, loss_local), 'dp'), 'blk')  62.5 us
    psum x1, waiting for transfers between devices, on_device(): lax.psum((tower_query, tower_item, loss_local), 'dp')  61.4 us
    psum x1, blocking collectives, on_device(): lax.psum(lax.psum((tower_query, tower_item, loss_local), 'dp'), 'blk')  33.2 us
    all_gather x1, blocking collectives, on_device(): lax.all_gather(bucket_ids[0], 'blk', axis=0, tiled=True)  23.4 us
    all_gather x1, blocking collectives, on_device(): all_totals = lax.all_gather(log_total, 'blk', axis=0, tiled=True)  19.5 us
    dot_general x3, matrix products, contract_first(): lax.dot_general(left, right, (((0,), (0,)), ((), ())), preferred_element_...  18.9 us
    all_gather x1, blocking collectives, on_device(): lax.all_gather(own_ids, 'blk', axis=0, tiled=True)  18 us
    unnamed x13, local copies, waits for them, and re-layouts  9.76 us
  transfers between devices with their start and end apart: 4, of which 3 were waited for; matrix products, arithmetic and copies ran while one was open for 8% of the time, Pallas kernels for 0%

profile of v1, /device:TPU:0, one launch (start us, length us, event | category | flops | bytes accessed | tf_op | source)
XLA Modules:
  0.0 300.9 jit_solution(2312098372734600482)
XLA Ops:
  7.2 0.0 copy-start
  7.2 0.0 all-gather.6.cloned.1.call-start
  7.2 1.1 copy-done
  8.3 2.1 convolution_convert_fusion
  10.4 0.0 all-gather.6.cloned.1.call-update
  10.4 0.0 all-gather.8.cloned.1.call-start
  10.5 2.3 convolution_convert_fusion.1
  12.8 0.0 all-gather.8.cloned.1.call-update
  12.8 0.0 all-reduce.7.cloned.1.call-start
  12.9 0.7 reduce
  13.6 23.4 %all-gather.1 = s32[1,6144]{1,0:T(1,128)S(1)} all-gather(s32[1,384]{1,0:T(1,128)} %param.10), channel_id=3, replica_groups=mesh['blk'=16,'dp'=2] {'blk'}, dimensions={1}, use_global_device_ids=true | all-gather | bytes 26112 | tf_op jit(solution)/shard_map/all_gather | solution.py:38
  37.0 4.4 %select_reduce_fusion = f32[6144]{0:T(1024)S(1)} fusion(f32[256]{0:T(256)} %param.11, s32[6144]{0:T(1024)S(1)} %bitcast.30), kind=kLoop, calls=%fused_computation.10 | loop fusion | flops 4712448 | bytes 50176 | tf_op jit(solution)/shard_map/reduce_sum | solution.py:42
  41.4 0.1 dynamic_slice.6
  41.5 18.0 %all-gather = s32[1,6144]{1,0:T(1,128)S(1)} all-gather(s32[1,384]{1,0:T(1,128)} %param.9), channel_id=2, replica_groups=mesh['blk'=16,'dp'=2] {'blk'}, dimensions={1}, use_global_device_ids=true | all-gather | bytes 26112 | tf_op jit(solution)/shard_map/all_gather | solution.py:37
  59.5 0.0 all-gather.6.cloned.1.call-done
  59.5 5.1 %fusion.3 = (f32[384]{0:T(512)S(1)}, f32[384,6144]{1,0:T(8,128)S(1)}) fusion(s32[384]{0:T(512)S(1)} %iota_add_fusion, s32[6144]{0:T(1024)S(1)} %bitcast.26, s32[384]{0:T(512)S(1)} %reduce, f32[6144]{0:T(1024)S(1)} %select_reduce_fusion, bf16[384,256]{1,0:T(8,128)(2,1)} %convolution_convert_fusion.1, bf16[6144,256]{1,0:T(8,128)(2,1)} %all-gather.6.cloned.1.call-done), kind=kOutput, calls=%fused_computation.12 | convolution fusion | flops 1224474240 | bytes 12833280 | tf_op jit(solution)/shard_map/dot_general | solution.py:11
  64.6 0.0 copy-start.1
  64.6 0.0 copy-start.3
  64.6 0.0 copy-start.4
  64.6 3.6 %copy-done.1 = f32[384,6144]{1,0:T(8,128)} copy-done((f32[384,6144]{1,0:T(8,128)}, f32[384,6144]{1,0:T(8,128)S(1)}, u32[]{:S(2)}) %copy-start.1) | copy-done | bytes 9437208
  68.2 0.1 constant_dynamic-slice_fusion
  68.3 3.4 %gather_fusion = f32[384]{0:T(512)S(1)} fusion(f32[384,384]{1,0:T(8,128)S(1)} %constant_dynamic-slice_fusion, s32[384]{0:T(512)S(1)} %or_reduce_fusion), kind=kCustom, calls=%fused_computation | custom fusion | bytes 6144 | tf_op jit(solution)/shard_map/jit(diagonal)/cond/branch_0_fun/gather | solution.py:54
  71.7 6.0 %exponential_reduce_fusion = f32[384]{0:T(512)S(1)} fusion(f32[384,6144]{1,0:T(8,128)} %copy-done.1, f32[384]{0:T(512)S(1)} %get-tuple-element.21, s32[384]{0:T(512)S(1)} %iota_add_fusion, s32[6144]{0:T(1024)S(1)} %bitcast.27, s32[384]{0:T(512)S(1)} %reduce), kind=kLoop, calls=%fused_computation.4 | loop fusion | flops 14155392 | bytes 9467904 | tf_op jit(solution)/shard_map/reduce_sum | solution.py:52
  77.7 0.6 subtract_reduce_fusion
  78.3 19.5 %all-gather.2 = f32[16,1,384]{2,1,0:T(1,128)S(1)} all-gather(f32[1,1,384]{2,1,0:T(1,128)S(1)} %reshape.37), channel_id=1, replica_groups=mesh['blk'=16,'dp'=2] {'blk'}, dimensions={0}, use_global_device_ids=true | all-gather | bytes 26112 | tf_op jit(solution)/shard_map/all_gather | solution.py:64
  97.8 8.1 %all-gather.8.cloned.1.call-done = bf16[6144,256]{1,0:T(8,128)(2,1)} async-done(((bf16[384,256]{1,0:T(8,128)(2,1)}), bf16[6144,256]{1,0:T(8,128)(2,1)}) %all-gather.8.cloned.1.call-update) | async-done | bytes 3145744 | tf_op jit(solution)/shard_map/all_gather | solution.py:66
  105.9 0.0 copy-done.3
  105.9 0.0 copy-done.4
  105.9 0.0 copy-start.2
  105.9 8.5 %fusion.11 = bf16[384,256]{1,0:T(8,128)(2,1)S(1)} fusion(bf16[6144,256]{1,0:T(8,128)(2,1)} %all-gather.8.cloned.1.call-done, bf16[384,256]{1,0:T(8,128)(2,1)S(1)} %copy-done.3, f32[6144]{0:T(1024)S(1)} %bitcast.31, f32[384]{0:T(512)S(1)} %dynamic_slice.6, s32[384]{0:T(512)S(1)} %iota_add_fusion, s32[384]{0:T(512)S(1)} %reduce, s32[6144]{0:T(1024)S(1)} %bitcast.28, ...), kind=kOutput, calls=%fused_computation.24 | convolution fusion | flops 2435186688 | bytes 3789312 | tf_op jit(solution)/shard_map/dot_general | solution.py:17
  114.4 1.4 convolution_bitcast_fusion
  115.8 0.0 copy-done.2
  115.8 9.0 %convolution_bitcast_fusion.1 = f32[1024,256]{0,1:T(8,128)} fusion(bf16[6144,256]{1,0:T(8,128)(2,1)} %all-gather.6.cloned.1.call-done, f32[384,6144]{1,0:T(8,128)} %copy-done.1, f32[384]{0:T(512)S(1)} %get-tuple-element.20, s32[384]{0:T(512)S(1)} %iota_add_fusion, s32[6144]{0:T(1024)S(1)} %bitcast.29, s32[384]{0:T(512)S(1)} %reduce, ...), kind=kOutput, calls=%fused_computation.16 | convolution fusion | flops 1423835136 | bytes 14643712 | tf_op jit(solution)/shard_map/dot_general | solution.py:17
  124.8 0.0 all-reduce.7.cloned.1.call-update
  124.9 0.0 all-reduce.5.cloned.1.call-start
  124.9 61.4 %all-reduce.7.cloned.1.call-done = (f32[1024,256]{0,1:T(8,128)}, f32[1024,256]{0,1:T(8,128)}) async-done(((f32[1024,256]{0,1:T(8,128)}, f32[1024,256]{0,1:T(8,128)}), (f32[1024,256]{0,1:T(8,128)}, f32[1024,256]{0,1:T(8,128)})) %all-reduce.7.cloned.1.call-update) | async-done | bytes 2097168 | tf_op jit(solution)/shard_map/psum | solution.py:79
  186.3 0.0 all-reduce.5.cloned.1.call-update
  186.3 5.6 %psum.46 = f32[]{:T(128)} all-reduce(f32[]{:T(128)} %get-tuple-element.19), channel_id=1, replica_groups=mesh['blk'=16,'dp'=2] {'dp'}, use_global_device_ids=true, to_apply=%region_8.9 | all-reduce | flops 1 | bytes 8 | tf_op jit(solution)/shard_map/psum | solution.py:79
  191.9 33.2 %psum.47 = f32[]{:T(128)} all-reduce(f32[]{:T(128)} %psum.46), channel_id=1, replica_groups=mesh['blk'=16,'dp'=2] {'blk'}, use_global_device_ids=true, to_apply=%region_9.10 | all-reduce | flops 1 | bytes 8 | tf_op jit(solution)/shard_map/psum | solution.py:78
  225.7 62.5 %all-reduce.5.cloned.1.call-done = (f32[1024,256]{0,1:T(8,128)}, f32[1024,256]{0,1:T(8,128)}) async-done(((f32[1024,256]{0,1:T(8,128)}, f32[1024,256]{0,1:T(8,128)}), (f32[1024,256]{0,1:T(8,128)}, f32[1024,256]{0,1:T(8,128)})) %all-reduce.5.cloned.1.call-update) | async-done | bytes 2097168 | tf_op jit(solution)/shard_map/psum | solution.py:78
  288.2 2.5 copy.16
  290.7 2.5 copy.17
  (3 shorter events, 0.0 us)
Async XLA Ops:
  7.2 1.1 copy-start
  7.2 52.3 %all-gather.6.cloned.1.call-start = ((), (), s32[]{:S(2)}) async-start(), calls=%async_computation | async-start | bytes 3342336 | tf_op jit(solution)/shard_map/all_gather | solution.py:35
  10.4 95.5 %all-gather.8.cloned.1.call-start = ((), (), s32[]{:S(2)}) async-start(), calls=%async_computation.1 | async-start | bytes 3342336 | tf_op jit(solution)/shard_map/all_gather | solution.py:66
  12.8 173.5 %all-reduce.7.cloned.1.call-start = ((), (), s32[]{:S(2)}) async-start(), calls=%async_computation.3 | async-start | bytes 4194304 | tf_op jit(solution)/shard_map/psum | solution.py:79
  64.6 3.6 %copy-start.1 = (f32[384,6144]{1,0:T(8,128)}, f32[384,6144]{1,0:T(8,128)S(1)}, u32[]{:S(2)}) copy-start(f32[384,6144]{1,0:T(8,128)S(1)} %get-tuple-element.22) | copy-start | bytes 28311556
  64.6 41.3 %copy-start.3 = (bf16[384,256]{1,0:T(8,128)(2,1)S(1)}, bf16[384,256]{1,0:T(8,128)(2,1)}, u32[]{:S(2)}) copy-start(bf16[384,256]{1,0:T(8,128)(2,1)} %convolution_convert_fusion) | copy-start | bytes 589828
  64.6 41.3 %copy-start.4 = (bf16[384,256]{1,0:T(8,128)(2,1)S(1)}, bf16[384,256]{1,0:T(8,128)(2,1)}, u32[]{:S(2)}) copy-start(bf16[384,256]{1,0:T(8,128)(2,1)} %convolution_convert_fusion.1) | copy-start | bytes 589828
  105.9 9.9 %copy-start.2 = (bf16[1,384,1024]{2,1,0:T(8,128)(2,1)S(1)}, bf16[1,384,1024]{2,1,0:T(8,128)(2,1)}, u32[]{:S(2)}) copy-start(bf16[1,384,1024]{2,1,0:T(8,128)(2,1)} %param.7) | copy-start | bytes 2359300
  124.9 163.3 %all-reduce.5.cloned.1.call-start = ((), (), s32[]{:S(2)}) async-start(), calls=%async_computation.2 | async-start | bytes 4194304 | tf_op jit(solution)/shard_map/psum | solution.py:78
Sparse Core Ops, SparseCore 0:
  10.8 48.2 all-gather.5
  62.0 43.8 all-gather.7
  125.0 61.2 all-reduce.6
  189.8 98.3 all-reduce.4
